TPU v7x, 32 devices: a whole 2x2x4 slice. The times are simulated.
32 devices in a mesh: seq: 8 (over y, x, core), exp: 4 (over z).
Axes of the slice: x: 2, y: 2, z: 4, core: 2. Of those that a mesh axis runs over, the one named last changes fastest.
Arguments:
- queries: bfloat16 [2048, 4096], P('seq', 'exp'), may hold values from -6 to 6
- key_rows: bfloat16 [2048, 512], P('seq'), may hold values from -6 to 6
- value_rows: bfloat16 [2048, 512], P('seq'), may hold values from -6 to 6
- sink_logits: float32 [64], P('exp'), may hold values from -2 to 2
- residual: bfloat16 [2048, 2880], P('seq'), may hold values from -6 to 6
- out_weight: bfloat16 [4096, 2880], P('exp'), may hold values from -0.375 to 0.375
- norm_gain: float32 [2880], replicated, may hold values from 0.25 to 1.75
- expert_ids: int32 [2048, 4], P('seq'), may hold values from 0 to 31, all different within a row; in each aligned block of 256 rows (0 to 255, 256 to 511, ...) at most 48 rows name the same one
- route_gates: float32 [2048, 4], P('seq'), may hold values from 0.1 to 0.6
- gate_proj: bfloat16 [32, 2880, 2048], P('seq', None, 'exp'), may hold values from -0.109375 to 0.109375
- up_proj: bfloat16 [32, 2880, 2048], P('seq', None, 'exp'), may hold values from -0.109375 to 0.109375
- down_proj: bfloat16 [32, 2048, 2880], P('seq', 'exp'), may hold values from -0.125 to 0.125
Outputs:
- layer_out: bfloat16 [2048, 2880], P('seq')
Inputs may be any that keep to these rules, and one draw needn't show every extreme that they name: `expert_ids`: each token names 4 different experts. In each slab of 256 tokens no expert is named by more than 48 entries, and that bound is reached.
All inputs are finite; a program needn't handle non-finite values.
Results may differ from a plain program's by a relative error of at most 0.018.
Values may be sent and summed in bfloat16 or wider, within the bound.
No kernel may reach another device: no remote copies, remote signals or barrier semaphores. Data moves between devices by JAX's collectives and lax.ppermute only.
A program may use at most 128 MiB of HBM per device.

v0:
```python
import math

import jax
import jax.numpy as jnp
from jax import lax
from jax.sharding import PartitionSpec as P

HQ = 64
HK = 8
HEAD = 64
TOP = 4
WIN = 128


def passed_along(x, axis, by):
    count = lax.axis_size(axis)
    pairs = [(i, i + by) for i in range(count) if 0 <= i + by < count]
    return lax.ppermute(x, axis, pairs)


def normalize(mixed, gain):
    wide_vals = mixed.astype(jnp.float32)
    inv_scale = lax.rsqrt(jnp.mean(wide_vals * wide_vals, axis=-1, keepdims=True) + 1e-05)
    return (wide_vals * inv_scale * gain).astype(jnp.bfloat16)


def activate(gate_acc, up_acc):
    gate_acc = jnp.minimum(gate_acc, 7.0)
    up_acc = jnp.clip(up_acc, -7.0, 7.0)
    return ((up_acc + 1.0) * gate_acc * jax.nn.sigmoid(1.702 * gate_acc)).astype(jnp.bfloat16)


def send_back(partial_out):
    return lax.all_to_all(partial_out, "seq", split_axis=0, concat_axis=0, tiled=True)


def on_device(
    queries,
    key_rows,
    value_rows,
    sink_logits,
    residual,
    out_weight,
    norm_gain,
    expert_ids,
    route_gates,
    gate_proj,
    up_proj,
    down_proj,
):
    tok_rows = queries.shape[0]
    local_heads = queries.shape[1] // HEAD
    per_group = HQ // HK
    column = lax.axis_index("exp")
    slab_index = lax.axis_index("seq")
    tail_rows = passed_along((key_rows[tok_rows - WIN :], value_rows[tok_rows - WIN :]), "seq", 1)
    key_full = jnp.concatenate([tail_rows[0], key_rows], 0)
    value_full = jnp.concatenate([tail_rows[1], value_rows], 0)
    kv_count = max(1, local_heads // per_group)
    kv_start = column * local_heads // per_group
    key_sel = lax.dynamic_slice_in_dim(key_full, kv_start * HEAD, kv_count * HEAD, 1).reshape(
        WIN + tok_rows, kv_count, HEAD
    )
    value_sel = lax.dynamic_slice_in_dim(value_full, kv_start * HEAD, kv_count * HEAD, 1).reshape(
        WIN + tok_rows, kv_count, HEAD
    )
    key_heads = jnp.repeat(key_sel, local_heads // kv_count, axis=1)
    value_heads = jnp.repeat(value_sel, local_heads // kv_count, axis=1)
    query_heads = queries.reshape(tok_rows, local_heads, HEAD)
    scores = jnp.einsum(
        "qhd,khd->hqk", query_heads, key_heads, preferred_element_type=jnp.float32
    ) * (1.0 / math.sqrt(HEAD))
    first_pos = slab_index * tok_rows
    q_pos = first_pos + jnp.arange(tok_rows, dtype=jnp.int32)
    k_pos = first_pos - WIN + jnp.arange(WIN + tok_rows, dtype=jnp.int32)
    allowed = (
        (k_pos[None, :] <= q_pos[:, None])
        & (k_pos[None, :] > q_pos[:, None] - WIN)
        & (k_pos[None, :] >= 0)
    )
    scores = jnp.where(allowed[None], scores, -1e30)
    row_top = jnp.maximum(jnp.max(scores, axis=-1), sink_logits[:, None])
    expo = jnp.exp(scores - row_top[..., None])
    denominator = jnp.sum(expo, axis=-1) + jnp.exp(sink_logits[:, None] - row_top)
    weights = (expo / denominator[..., None]).astype(jnp.bfloat16)
    context = jnp.einsum("hqk,khd->qhd", weights, value_heads, preferred_element_type=jnp.float32)
    context = context.astype(jnp.bfloat16).reshape(tok_rows, local_heads * HEAD)
    attn_part = jnp.dot(context, out_weight, preferred_element_type=jnp.float32)
    attn_out = lax.psum(attn_part.astype(jnp.bfloat16), "exp").astype(jnp.float32)
    mixed = (residual.astype(jnp.float32) + attn_out).astype(jnp.bfloat16)
    normed = normalize(mixed, norm_gain)
    local_experts = gate_proj.shape[0]
    seq_count = lax.axis_size("seq")
    experts = local_experts * seq_count
    cap = 3 * tok_rows * TOP // (2 * experts)
    flat_ids = expert_ids.reshape(-1)
    onehot = (flat_ids[:, None] == jnp.arange(experts, dtype=jnp.int32)[None, :]).astype(jnp.int32)
    rank_ids = jnp.cumsum(onehot, axis=0) - 1
    slot_ids = jnp.sum(rank_ids * onehot, axis=1)
    targets = flat_ids * cap + slot_ids
    source = (
        jnp.full((experts * cap,), -1, jnp.int32)
        .at[targets]
        .set(jnp.arange(tok_rows * TOP, dtype=jnp.int32))
    )
    filled = source >= 0
    token_of = jnp.where(filled, source // TOP, 0)
    packed = jnp.where(filled[:, None], normed[token_of], jnp.zeros((), jnp.bfloat16))
    packed = packed.reshape(seq_count, local_experts, cap, packed.shape[1])
    slot_block = lax.all_to_all(packed, "seq", split_axis=0, concat_axis=0, tiled=True)
    gate_acc = jnp.einsum(
        "secd,edf->secf", slot_block, gate_proj, preferred_element_type=jnp.float32
    )
    up_acc = jnp.einsum("secd,edf->secf", slot_block, up_proj, preferred_element_type=jnp.float32)
    hidden = activate(gate_acc, up_acc)
    partial_out = jnp.einsum(
        "secf,efd->secd", hidden, down_proj, preferred_element_type=jnp.float32
    ).astype(jnp.bfloat16)
    returned = send_back(partial_out)
    flat_back = returned.reshape(experts * cap, returned.shape[3])
    picked = flat_back[targets].astype(jnp.float32).reshape(tok_rows, TOP, returned.shape[3])
    moe_part = jnp.sum(picked * route_gates[:, :, None], axis=1)
    moe_total = lax.psum(moe_part.astype(jnp.bfloat16), "exp").astype(jnp.float32)
    return (mixed.astype(jnp.float32) + moe_total).astype(jnp.bfloat16)


def solution(mesh):
    return jax.shard_map(
        on_device,
        mesh=mesh,
        in_specs=(
            P("seq", "exp"),
            P("seq", None),
            P("seq", None),
            P("exp"),
            P("seq", None),
            P("exp", None),
            P(),
            P("seq", None),
            P("seq", None),
            P("seq", None, "exp"),
            P("seq", None, "exp"),
            P("seq", "exp", None),
        ),
        out_specs=P("seq", None),
        check_vma=False,
    )
```

profile of v0, /device:TPU:0, one launch (start us, length us, event | category | flops | bytes accessed | tf_op | source)
XLA Modules:
  0.0 490.9 jit_solution(17000879726990908606)
XLA Ops:
  6.5 1.1 copy.33
  7.7 2.4 collective-permute-start
  10.1 1.1 copy.35
  11.2 4.5 collective-permute-start.1
  15.8 1.2 copy.37
  17.0 0.8 copy.40
  18.3 1.2 fusion.11
  19.6 1.3 fusion.10
  21.1 1.8 fusion.34
  22.9 0.8 slice-done.1
  23.7 2.9 convolution_convert_fusion
  26.7 9.0 %reduce-window.6 = s32[32,8,128]{2,1,0:T(8,128)S(1)} reduce-window(s32[32,8,128]{2,1,0:T(8,128)S(1)} %fusion.37, s32[]{:T(128)} %constant.27.clone.1), window={size=1x1x128 pad=0_0x0_0x127_0}, to_apply=%region_3.4 | reduce-window | flops 4161536 | bytes 262148 | tf_op jit(solution)/shard_map/reduce-window
  36.5 4.5 scatter_custom_fusion
  41.2 52.9 %all-reduce.3.cloned.1.call-done = bf16[256,2880]{0,1:T(8,128)(2,1)} async-done(((bf16[256,2880]{0,1:T(8,128)(2,1)}), bf16[256,2880]{0,1:T(8,128)(2,1)}) %all-reduce.3.cloned.1.call-update) | async-done | bytes 1474576 | tf_op jit(solution)/shard_map/psum | solution.py:89
  94.1 1.9 fusion.13
  96.0 3.0 fusion.15
  99.1 1.8 copy.44
  100.9 8.1 %gather_fusion = bf16[1536,2880]{1,0:T(8,128)(2,1)} fusion(bf16[256,2880]{1,0:T(8,128)(2,1)S(1)} %copy.44, s32[2048]{0:T(1024)S(1)} %pad_clamp_fusion), kind=kCustom, calls=%fused_computation | custom fusion | bytes 17700864 | tf_op jit(solution)/shard_map/gather | solution.py:108
  109.0 8.0 %broadcast_select_fusion = bf16[8,4,48,2880]{3,2,1,0:T(8,128)(2,1)} fusion(bf16[8,4,48,2880]{3,2,1,0:T(8,128)(2,1)} %bitcast.70, pred[8,4,48]{2,1,0:T(4,128)(4,1)S(1)} %broadcast_in_dim.62), kind=kLoop, calls=%fused_computation.11 | loop fusion | flops 4423680 | bytes 17696256 | tf_op jit(solution)/shard_map/jit(_where)/select_n | solution.py:108
  117.0 104.8 %all_to_all.10 = bf16[8,4,48,2880]{3,2,1,0:T(8,128)(2,1)S(1)} all-to-all(bf16[8,4,48,2880]{3,2,1,0:T(8,128)(2,1)} %broadcast_select_fusion), channel_id=1, replica_groups=mesh['seq'=8,'exp'=4] {'seq'}, dimensions={0} | all-to-all | bytes 17694720 | tf_op jit(solution)/shard_map/all_to_all | solution.py:110
  221.8 3.5 copy-done.2
  225.3 9.6 %fusion.2 = f32[4,8,48,512]{3,2,1,0:T(8,128)} fusion(bf16[4,2880,512]{2,1,0:T(8,128)(2,1)} %param.21, bf16[8,4,48,2880]{3,2,1,0:T(8,128)(2,1)S(1)} %all_to_all.10), kind=kOutput, calls=%fused_computation.6 | convolution fusion | flops 4529848320 | bytes 23789568 | tf_op jit(solution)/shard_map/secd,edf->secf/dot_general | solution.py:111
  235.0 25.9 %convert_bitcast_fusion = bf16[8,4,48,2880]{3,2,0,1:T(8,128)(2,1)} fusion(bf16[4,512,2880]{1,2,0:T(8,128)(2,1)} %param.23, f32[4,8,48,512]{3,2,1,0:T(8,128)} %fusion.2, bf16[4,2880,512]{2,1,0:T(8,128)(2,1)} %param.22, bf16[8,4,48,2880]{3,2,1,0:T(8,128)(2,1)} %copy-done.2), kind=kOutput, calls=%fused_computation.10 | convolution fusion | flops 9071984640 | bytes 44433408 | tf_op jit(solution)/shard_map/secf,efd->secd/dot_general | solution.py:116
  260.8 7.9 %copy.47 = bf16[8,4,48,2880]{3,2,1,0:T(8,128)(2,1)} copy(bf16[8,4,48,2880]{3,2,0,1:T(8,128)(2,1)} %convert_bitcast_fusion) | data formatting | bytes 17694720 | tf_op jit(solution)/shard_map/convert_element_type | solution.py:118
  268.7 5.1 %all-to-all-start.1 = ((bf16[8,4,48,2880]{3,2,1,0:T(8,128)(2,1)}), bf16[8,4,48,2880]{3,2,1,0:T(8,128)(2,1)}, u32[]{:S(2)}, u32[]{:S(2)}) async-start(bf16[8,4,48,2880]{3,2,1,0:T(8,128)(2,1)} %copy.47), calls=%async_computation.1 | async-start | bytes 18087936 | tf_op jit(solution)/shard_map/all_to_all | solution.py:34
  274.3 100.6 %all-to-all-done.1 = bf16[8,4,48,2880]{3,2,1,0:T(8,128)(2,1)} async-done(((bf16[8,4,48,2880]{3,2,1,0:T(8,128)(2,1)}), bf16[8,4,48,2880]{3,2,1,0:T(8,128)(2,1)}, u32[]{:S(2)}, u32[]{:S(2)}) %all-to-all-start.1) | async-done | bytes 8847392 | tf_op jit(solution)/shard_map/all_to_all | solution.py:34
  374.9 16.4 %gather_fusion.1 = bf16[1024,2880]{1,0:T(8,128)(2,1)} fusion(bf16[1536,2880]{1,0:T(8,128)(2,1)} %bitcast.21, s32[1024]{0:T(1024)S(1)} %broadcast_clamp_fusion), kind=kCustom, calls=%fused_computation.1 | custom fusion | bytes 11800576 | tf_op jit(solution)/shard_map/gather | solution.py:121
  391.3 11.7 %reshape.236 = f32[256,4,2880]{2,1,0:T(4,128)} reshape(bf16[1024,2880]{1,0:T(8,128)(2,1)} %gather_fusion.1) | data formatting | bytes 17694720 | tf_op jit(solution)/shard_map/convert_element_type | solution.py:121
  403.0 12.1 %multiply_reduce_fusion = bf16[256,2880]{1,0:T(8,128)(2,1)} fusion(f32[256,4,2880]{2,1,0:T(4,128)} %reshape.236, f32[256,4]{1,0:T(8,128)S(1)} %copy.48), kind=kLoop, calls=%fused_computation.3 | loop fusion | flops 5160960 | bytes 13275136 | tf_op jit(solution)/shard_map/reduce_sum | solution.py:122
  415.1 2.5 copy.49
  417.7 63.3 %all-reduce.5.cloned.1.call-done = bf16[256,2880]{0,1:T(8,128)(2,1)} async-done(((bf16[256,2880]{0,1:T(8,128)(2,1)}), bf16[256,2880]{0,1:T(8,128)(2,1)}) %all-reduce.5.cloned.1.call-update) | async-done | bytes 1474576 | tf_op jit(solution)/shard_map/psum | solution.py:123
  481.0 3.0 fusion.16
  (56 shorter events, 2.2 us)
Async XLA Ops:
  6.5 87.5 %all-reduce.3.cloned.1.call-start = ((), (), s32[]{:S(2)}) async-start(), calls=%async_computation.2 | async-start | bytes 2949120 | tf_op jit(solution)/shard_map/psum | solution.py:89
  7.6 11.8 %copy-start.6 = (f32[16]{0:T(128)S(1)}, f32[16]{0:T(128)}, u32[]{:S(2)}) copy-start(f32[16]{0:T(128)} %param.15) | copy-start | bytes 196
  7.7 10.5 %collective-permute-start = (bf16[128,512]{0,1:T(8,128)(2,1)S(1)}, bf16[128,512]{0,1:T(8,128)(2,1)S(1)}, u32[]{:S(2)}, u32[]{:S(2)}) collective-permute-start(bf16[128,512]{0,1:T(8,128)(2,1)S(1)} %slice.20), channel_id=1, source_target_pairs={{0,4},{4,8},{8,12},{12,16},{16,20},{20,24},{24,28},{1,5},{5,9},{9,... | collective-permute-start | bytes 393224 | tf_op jit(solution)/shard_map/ppermute | solution.py:18
  11.2 7.0 %collective-permute-start.1 = (bf16[128,512]{0,1:T(8,128)(2,1)S(1)}, bf16[128,512]{0,1:T(8,128)(2,1)S(1)}, u32[]{:S(2)}, u32[]{:S(2)}) collective-permute-start(bf16[128,512]{0,1:T(8,128)(2,1)S(1)} %slice.21), channel_id=1, source_target_pairs={{0,4},{4,8},{8,12},{12,16},{16,20},{20,24},{24,28},{1,5},{5,9},{9,... | collective-permute-start | bytes 393224 | tf_op jit(solution)/shard_map/ppermute | solution.py:18
  20.9 2.0 slice-start
  21.0 2.6 slice-start.1
  23.7 12.4 %copy-start.3 = (s32[256,4]{0,1:T(4,128)S(1)}, s32[256,4]{0,1:T(4,128)}, u32[]{:S(2)}) copy-start(s32[256,4]{0,1:T(4,128)} %param.19) | copy-start | bytes 12292
  23.7 70.4 %copy-start = (bf16[256,2880]{0,1:T(8,128)(2,1)S(1)}, bf16[256,2880]{0,1:T(8,128)(2,1)}, u32[]{:S(2)}) copy-start(bf16[256,2880]{0,1:T(8,128)(2,1)} %param.16) | copy-start | bytes 4423684
  26.5 69.5 %copy-start.4 = (f32[2880]{0:T(1024)S(1)}, f32[2880]{0:T(1024)}, u32[]{:S(2)}) copy-start(f32[2880]{0:T(1024)} %param.18) | copy-start | bytes 34564
  221.8 3.5 copy-start.2
  268.7 5.4 %copy-start.5 = (f32[256,4]{0,1:T(4,128)S(1)}, f32[256,4]{0,1:T(4,128)}, u32[]{:S(2)}) copy-start(f32[256,4]{0,1:T(4,128)} %param.20) | copy-start | bytes 12292
  268.7 106.2 %all-to-all-start.1 = ((bf16[8,4,48,2880]{3,2,1,0:T(8,128)(2,1)}), bf16[8,4,48,2880]{3,2,1,0:T(8,128)(2,1)}, u32[]{:S(2)}, u32[]{:S(2)}) async-start(bf16[8,4,48,2880]{3,2,1,0:T(8,128)(2,1)} %copy.47), calls=%async_computation.1 | async-start | bytes 18087936 | tf_op jit(solution)/shard_map/all_to_all | solution.py:34
  273.8 207.2 %all-reduce.5.cloned.1.call-start = ((), (), s32[]{:S(2)}) async-start(), calls=%async_computation.3 | async-start | bytes 2949120 | tf_op jit(solution)/shard_map/psum | solution.py:123
  403.0 78.0 %copy-start.1 = (bf16[256,2880]{0,1:T(8,128)(2,1)S(1)}, bf16[256,2880]{0,1:T(8,128)(2,1)}, u32[]{:S(2)}) copy-start(bf16[256,2880]{0,1:T(8,128)(2,1)} %all-reduce.3.cloned.1.call-done) | copy-start | bytes 4423684
Sparse Core Ops, SparseCore 0:
  26.7 67.3 all-reduce.2
  417.8 63.1 all-reduce.4
where the time goes:
time: 492 us; the launch traced here: 491 us
  waiting for transfers between devices  217 us (44%)
  blocking collectives  105 us (21%)
  local copies, waits for them, and re-layouts  62.8 us (13%)
  matrix products  41.4 us (8%)
  other arithmetic  39 us (8%)
  between operations  13.8 us (3%)
  starting transfers between devices  12.3 us (2%)
    all_to_all x1, blocking collectives, on_device(): lax.all_to_all(packed, 'seq', split_axis=0, concat_axis=0, tiled=True)  105 us
    all_to_all x1, waiting for transfers between devices, send_back(): lax.all_to_all(partial_out, 'seq', split_axis=0, concat_axis=0, tiled=True)  101 us
    psum x1, waiting for transfers between devices, on_device(): lax.psum(moe_part.astype(jnp.bfloat16), 'exp').astype(jnp.float32)  63.3 us
    psum x1, waiting for transfers between devices, on_device(): lax.psum(attn_part.astype(jnp.bfloat16), 'exp').astype(jnp.float32)  52.9 us
    dot_general x1, matrix products, on_device(): jnp.einsum('secf,efd->secd', hidden, down_proj, preferred_element_type=jn...  25.9 us
    gather x1, local copies, waits for them, and re-layouts, on_device(): flat_back[targets].astype(jnp.float32)  16.4 us
    reduce_sum x1, other arithmetic, on_device(): moe_part = jnp.sum(picked * route_gates[:, :, None], axis=1)  12.1 us
    convert_element_type x1, local copies, waits for them, and re-layouts, on_device(): flat_back[targets].astype(jnp.float32)  11.7 us
  transfers between devices with their start and end apart: 5, of which 3 were waited for; matrix products, arithmetic and copies ran while one was open for 4% of the time, Pallas kernels for 0%

commit v1 on v0

v1 whole, which is shorter than its diff:
```python
import functools
import math

import jax
import jax.numpy as jnp
from jax import lax
from jax.experimental import pallas as pl
from jax.experimental.pallas import tpu as pltpu
from jax.sharding import PartitionSpec as P

HQ = 64
HK = 8
HEAD = 64
TOP = 4
WIN = 128
LANES = 128
F32 = jnp.float32
BF16 = jnp.bfloat16
VMEM_BYTES = 56 * 1024 * 1024


def params(*semantics):
    return pltpu.CompilerParams(dimension_semantics=semantics, vmem_limit_bytes=VMEM_BYTES)


def cost(flops, nbytes):
    return pl.CostEstimate(flops=int(flops), bytes_accessed=int(nbytes), transcendentals=0)


def full(shape):
    zeros = (0,) * len(shape)
    return pl.BlockSpec(shape, lambda *_: zeros)


def swap(x, axis, bit):
    count = lax.axis_size(axis)
    return lax.ppermute(x, axis, [(i, i ^ bit) for i in range(count)])


def route_kernel(first_ref, meta_ref, place_ref, turned_ref, gate_ref, *, slabs, experts, cap, rows):
    first = first_ref[0].astype(F32)
    masks, gates = [], []
    for n in range(slabs):
        ids = meta_ref[n, 0:TOP, :]
        amounts = meta_ref[n, TOP : 2 * TOP, :]
        for e in range(experts):
            hit = ids == first + e
            masks.append(jnp.max(jnp.where(hit, 1.0, 0.0), axis=0, keepdims=True))
            gates.append(jnp.sum(jnp.where(hit, amounts, 0.0), axis=0, keepdims=True))
    mask = jnp.concatenate(masks, axis=0)
    before = lax.broadcasted_iota(jnp.int32, (rows, rows), 0) < lax.broadcasted_iota(
        jnp.int32, (rows, rows), 1
    )
    earlier = jnp.dot(
        mask.astype(BF16), jnp.where(before, 1.0, 0.0).astype(BF16), preferred_element_type=F32
    )
    slot = jnp.where(mask > 0.0, earlier, -1.0)
    wanted = lax.broadcasted_iota(jnp.int32, (cap, rows), 0).astype(F32)
    for n in range(slabs):
        pieces = []
        for e in range(experts):
            at = n * experts + e
            chosen = jnp.where(slot[at : at + 1, :] == wanted, 1.0, 0.0)
            pieces.append(chosen)
            row_gate = jnp.sum(chosen * gates[at], axis=1, keepdims=True)
            gate_ref[e, n * cap : (n + 1) * cap, :] = jnp.broadcast_to(row_gate, (cap, LANES))
        place = jnp.concatenate(pieces, axis=0)
        place_ref[n] = place.astype(BF16)
        turned_ref[n] = place.T.astype(BF16)


def route(first, meta, experts, cap):
    slabs, _, rows = meta.shape
    return pl.pallas_call(
        functools.partial(route_kernel, slabs=slabs, experts=experts, cap=cap, rows=rows),
        out_shape=(
            jax.ShapeDtypeStruct((slabs, experts * cap, rows), BF16),
            jax.ShapeDtypeStruct((slabs, rows, experts * cap), BF16),
            jax.ShapeDtypeStruct((experts, slabs * cap, LANES), F32),
        ),
        in_specs=[
            pl.BlockSpec(memory_space=pltpu.SMEM),
            pl.BlockSpec(memory_space=pltpu.VMEM),
        ],
        out_specs=[pl.BlockSpec(memory_space=pltpu.VMEM)] * 3,
        compiler_params=pltpu.CompilerParams(vmem_limit_bytes=VMEM_BYTES),
        cost_estimate=cost(4e9, 2e6),
        name="route",
    )(first, meta)


def attention_kernel(slab_ref, sink_ref, q_ref, k_ref, v_ref, out_ref, *, heads, kv_count):
    block = pl.program_id(0)
    span = 2 * WIN
    row = lax.broadcasted_iota(jnp.int32, (WIN, span), 0)
    key = lax.broadcasted_iota(jnp.int32, (WIN, span), 1)
    first_key = jnp.where((slab_ref[0] == 0) & (block == 0), WIN, 0)
    allowed = (key <= row + WIN) & (key > row) & (key >= first_key)
    begin = pl.multiple_of(block * WIN, WIN)
    per_kv = heads // kv_count
    for pair in range(heads // 2):
        kv = (2 * pair) // per_kv
        lanes = slice(pair * 2 * HEAD, (pair + 1) * 2 * HEAD)
        q = q_ref[:, lanes]
        spread = []
        for side in range(2):
            keys = k_ref[kv, side, pl.ds(begin, span), :]
            scores = lax.dot_general(
                q, keys, (((1,), (1,)), ((), ())), preferred_element_type=F32
            ) * (1.0 / math.sqrt(HEAD))
            scores = jnp.where(allowed, scores, -1e30)
            sink = sink_ref[2 * pair + side]
            row_top = jnp.maximum(jnp.max(scores, axis=-1, keepdims=True), sink)
            expo = jnp.exp(scores - row_top)
            denominator = jnp.sum(expo, axis=-1, keepdims=True) + jnp.exp(sink - row_top)
            spread.append((expo / denominator).astype(BF16))
        context = jnp.dot(
            spread[0], v_ref[kv, 0, pl.ds(begin, span), :], preferred_element_type=F32
        ) + jnp.dot(spread[1], v_ref[kv, 1, pl.ds(begin, span), :], preferred_element_type=F32)
        out_ref[:, lanes] = context.astype(BF16)


def attention(slab_index, sinks, queries, keys, values):
    rows, width = queries.shape
    heads = width // HEAD
    kv_count = keys.shape[0]
    return pl.pallas_call(
        functools.partial(attention_kernel, heads=heads, kv_count=kv_count),
        grid=(rows // WIN,),
        out_shape=jax.ShapeDtypeStruct((rows, width), BF16),
        in_specs=[
            pl.BlockSpec(memory_space=pltpu.SMEM),
            pl.BlockSpec(memory_space=pltpu.SMEM),
            pl.BlockSpec((WIN, width), lambda i: (i, 0)),
            full(keys.shape),
            full(values.shape),
        ],
        out_specs=pl.BlockSpec((WIN, width), lambda i: (i, 0)),
        compiler_params=params("arbitrary"),
        cost_estimate=cost(4e9, 2e6),
        name="attention",
    )(slab_index, sinks, queries, keys, values)


def both_sides(x, kv_count):
    rows = x.shape[0]
    heads = x.reshape(rows, kv_count, HEAD).transpose(1, 0, 2)
    zero = jnp.zeros_like(heads)
    return jnp.stack(
        [jnp.concatenate([heads, zero], 2), jnp.concatenate([zero, heads], 2)], axis=1
    )


def project_kernel(bit_ref, ctx_ref, w_ref, out_ref, *, width):
    out_ref[0] = jnp.dot(
        ctx_ref[...], w_ref[:, 0:width], preferred_element_type=F32
    ).astype(out_ref.dtype)


def project(bit, context, out_weight, start, width, block):
    rows, depth = context.shape
    half = rows // 2
    return pl.pallas_call(
        functools.partial(project_kernel, width=width),
        grid_spec=pltpu.PrefetchScalarGridSpec(
            num_scalar_prefetch=1,
            grid=(2,),
            in_specs=[
                pl.BlockSpec((half, depth), lambda i, bit_ref: (1 - i - bit_ref[0] + 2 * i * bit_ref[0], 0)),
                pl.BlockSpec((depth, block), lambda i, bit_ref: (0, start // block)),
            ],
            out_specs=pl.BlockSpec((1, half, width), lambda i, bit_ref: (i, 0, 0)),
        ),
        out_shape=jax.ShapeDtypeStruct((2, half, width), BF16),
        compiler_params=params("arbitrary"),
        cost_estimate=cost(2 * rows * depth * width, 2 * depth * width),
        name="project",
    )(bit, context, out_weight)


def enter_kernel(
    *refs, first, last, orders, slabs, experts, cap, rows, width
):
    refs = list(refs)
    near_ref, far_ref, place_ref, gain_ref, wg_ref, wu_ref = refs[:6]
    refs = refs[6:]
    if not first:
        acc_in, ss_in = refs[:2]
        refs = refs[2:]
    if last:
        hidden_ref, = refs[:1]
        refs = refs[1:]
        x_ref, ss_ref = refs
    else:
        acc_ref, ss_ref = refs[:2]
        x_ref, = refs[2:]
    e = pl.program_id(0)
    half = slabs // 2

    @pl.when(e == 0)
    def _():
        for n in range(slabs):
            source = near_ref if n < half else far_ref
            at = orders[n % half]
            x = jnp.dot(place_ref[n], source[at], preferred_element_type=F32)
            ss = jnp.sum(x * x, axis=1, keepdims=True)
            x = (x * gain_ref[...]).astype(BF16)
            for k in range(experts):
                part = slice(n * cap, (n + 1) * cap)
                x_ref[k, part, :] = x[k * cap : (k + 1) * cap]
                new = jnp.broadcast_to(ss[k * cap : (k + 1) * cap], (cap, LANES))
                if not first:
                    new = new + ss_in[k, part, :]
                ss_ref[k, part, :] = new

    x = x_ref[e]
    units = wg_ref.shape[2]
    gate_acc = jnp.dot(x, wg_ref[0], preferred_element_type=F32)
    up_acc = jnp.dot(x, wu_ref[0], preferred_element_type=F32)
    if not first:
        gate_acc = gate_acc + acc_in[0, :, 0:units]
        up_acc = up_acc + acc_in[0, :, units : 2 * units]
    if not last:
        acc_ref[0, :, 0:units] = gate_acc
        acc_ref[0, :, units : 2 * units] = up_acc
    else:
        total = last
        scale = lax.rsqrt(ss_ref[e][:, 0:1] * (1.0 / total) + 1e-05)
        gate_acc = jnp.minimum(gate_acc * scale, 7.0)
        up_acc = jnp.clip(up_acc * scale, -7.0, 7.0)
        hidden_ref[0] = (
            (up_acc + 1.0) * gate_acc / (1.0 + jnp.exp(-1.702 * gate_acc))
        ).astype(BF16)


def enter(near, far, place, gain, gate_proj, up_proj, carry, orders, start, last):
    half, rows, width = near.shape
    slabs, all_slots, _ = place.shape
    experts, total, units = gate_proj.shape
    cap = all_slots // experts
    slots = slabs * cap
    first = carry is None
    at = start // width
    weight_spec = pl.BlockSpec((1, width, units), lambda e: (e, at, 0))
    in_specs = [full(near.shape), full(far.shape), full(place.shape), full(gain.shape)]
    in_specs += [weight_spec, weight_spec]
    operands = [near, far, place, gain, gate_proj, up_proj]
    acc_spec = pl.BlockSpec((1, slots, 2 * units), lambda e: (e, 0, 0))
    ss_shape = (experts, slots, LANES)
    aliases = {}
    if not first:
        in_specs += [acc_spec, full(ss_shape)]
        operands += list(carry)
        if not last:
            aliases = {6: 0}
    scratch = [pltpu.VMEM((experts, slots, width), BF16)]
    if last:
        out_shape = jax.ShapeDtypeStruct((experts, slots, units), BF16)
        out_specs = pl.BlockSpec((1, slots, units), lambda e: (e, 0, 0))
        scratch += [pltpu.VMEM(ss_shape, F32)]
    else:
        out_shape = (
            jax.ShapeDtypeStruct((experts, slots, 2 * units), F32),
            jax.ShapeDtypeStruct(ss_shape, F32),
        )
        out_specs = (acc_spec, full(ss_shape))
    return pl.pallas_call(
        functools.partial(
            enter_kernel,
            first=first,
            last=total if last else 0,
            orders=orders,
            slabs=slabs,
            experts=experts,
            cap=cap,
            rows=rows,
            width=width,
        ),
        grid=(experts,),
        out_shape=out_shape,
        in_specs=in_specs,
        out_specs=out_specs,
        scratch_shapes=scratch,
        input_output_aliases=aliases,
        compiler_params=params("arbitrary"),
        cost_estimate=cost(4 * experts * slots * width * units * 1.5, 4 * experts * width * units),
        name="enter",
    )(*operands)


def leave_kernel(
    hidden_ref, w_ref, gate_ref, turned_ref, near_ref, far_ref, part_ref,
    *, orders, slabs, experts, cap, width
):
    e = pl.program_id(0)
    out = jnp.dot(hidden_ref[0], w_ref[0, :, 0:width], preferred_element_type=F32)
    out = (out * gate_ref[0][:, 0:1]).astype(BF16)
    for k in range(experts):

        @pl.when(e == k)
        def _():
            for n in range(slabs):
                part_ref[n, k * cap : (k + 1) * cap, :] = out[n * cap : (n + 1) * cap]

    @pl.when(e == experts - 1)
    def _():
        for n in range(slabs):
            target = near_ref if n < slabs // 2 else far_ref
            target[orders[n % (slabs // 2)]] = jnp.dot(
                turned_ref[n], part_ref[n], preferred_element_type=F32
            ).astype(BF16)


def leave(hidden, down_proj, row_gate, turned, orders, start, width, block):
    experts, slots, units = hidden.shape
    slabs, rows, all_slots = turned.shape
    cap = all_slots // experts
    half = slabs // 2
    piece = jax.ShapeDtypeStruct((half, rows, width), BF16)
    return pl.pallas_call(
        functools.partial(
            leave_kernel, orders=orders, slabs=slabs, experts=experts, cap=cap, width=width
        ),
        grid=(experts,),
        out_shape=(piece, piece),
        in_specs=[
            pl.BlockSpec((1, slots, units), lambda e: (e, 0, 0)),
            pl.BlockSpec((1, units, block), lambda e: (e, 0, start // block)),
            pl.BlockSpec((1, slots, LANES), lambda e: (e, 0, 0)),
            full(turned.shape),
        ],
        out_specs=(full(piece.shape), full(piece.shape)),
        scratch_shapes=[pltpu.VMEM((slabs, experts * cap, width), BF16)],
        compiler_params=params("arbitrary"),
        cost_estimate=cost(3 * experts * slots * width * units, 2 * experts * width * units),
        name="leave",
    )(hidden, down_proj, row_gate, turned)


def add(a, b):
    return (a.astype(F32) + b.astype(F32)).astype(BF16)


def gather_slabs(x, order):
    buf = x[None]
    for bit in order:
        buf = jnp.concatenate([buf, swap(buf, "seq", bit)], axis=0)
    return buf


def scatter_slabs(buf, order):
    for bit in reversed(order):
        half = buf.shape[0] // 2
        buf = add(buf[:half], swap(buf[half:], "seq", bit))
    return buf[0]


def positions(order, bits):
    found = []
    for p in range(1 << len(bits)):
        xor = sum(bit for k, bit in enumerate(bits) if p >> k & 1)
        found.append(sum(1 << k for k, bit in enumerate(order) if xor & bit))
    return tuple(found)


def sum_half(send, keep, n_exp):
    keep = add(keep, swap(send, "exp", 1))
    bit = 2
    while bit < n_exp:
        other = swap(keep, "exp", bit)
        bit *= 2
        if bit < n_exp:
            keep = add(keep, other)
        else:
            return keep.astype(F32) + other.astype(F32)
    return keep.astype(F32)


def chunks_of(total):
    block = -(-total // (4 * LANES)) * LANES
    return [(s, min(block, total - s)) for s in range(0, total, block)], block


def on_device(
    queries,
    key_rows,
    value_rows,
    sink_logits,
    residual,
    out_weight,
    norm_gain,
    expert_ids,
    route_gates,
    gate_proj,
    up_proj,
    down_proj,
):
    rows = queries.shape[0]
    half = rows // 2
    local_heads = queries.shape[1] // HEAD
    per_group = HQ // HK
    column = lax.axis_index("exp")
    slab_index = lax.axis_index("seq")
    n_exp = lax.axis_size("exp")
    slabs = lax.axis_size("seq")
    experts = gate_proj.shape[0]
    cap = 3 * rows * TOP // (2 * experts * slabs)
    total = residual.shape[1]
    low_bit = column % 2
    bit = low_bit[None].astype(jnp.int32)
    bits = [b for b in (1 << k for k in range(1, 31)) if b < slabs]

    kv_count = max(1, local_heads // per_group)
    kv_start = column * local_heads // per_group
    key_sel = lax.dynamic_slice_in_dim(key_rows, kv_start * HEAD, kv_count * HEAD, 1)
    value_sel = lax.dynamic_slice_in_dim(value_rows, kv_start * HEAD, kv_count * HEAD, 1)
    tail = jnp.concatenate([key_sel[rows - WIN :], value_sel[rows - WIN :]], axis=1)
    tail = lax.ppermute(tail, "seq", [(i, i + 1) for i in range(slabs - 1)])
    key_full = jnp.concatenate([tail[:, : kv_count * HEAD], key_sel], 0)
    value_full = jnp.concatenate([tail[:, kv_count * HEAD :], value_sel], 0)
    context = attention(
        slab_index[None].astype(jnp.int32),
        sink_logits,
        queries,
        both_sides(key_full, kv_count),
        both_sides(value_full, kv_count),
    )

    def halves(x):
        kept = lax.dynamic_slice_in_dim(x, low_bit * half, half, 0)
        other = lax.dynamic_slice_in_dim(x, (1 - low_bit) * half, half, 0)
        return kept, other

    meta = jnp.concatenate([expert_ids.astype(F32), route_gates], axis=1)
    meta = jnp.concatenate(halves(meta), axis=0).T
    meta = gather_slabs(meta, bits + [1])
    first_expert = (slab_index * experts)[None].astype(jnp.int32)
    place, turned, row_gate = route(first_expert, meta, experts, cap)

    chunks, block = chunks_of(total)
    res_kept = lax.dynamic_slice_in_dim(residual, low_bit * half, half, 0)
    gain = norm_gain[None, :]
    carry = None
    mixed_kept = []
    for c, (start, width) in enumerate(chunks):
        parts = project(bit, context, out_weight, start, width, block)
        attn = sum_half(parts[0], parts[1], n_exp)
        kept = (res_kept[:, start : start + width].astype(F32) + attn).astype(BF16)
        mixed_kept.append(kept)
        mixed = jnp.concatenate([kept, swap(kept, "exp", 1)], axis=0)
        order = bits if c % 2 == 0 else bits[::-1]
        near = gather_slabs(mixed, order)
        far = swap(near, "seq", 1)
        carry = enter(
            near, far, place, gain[:, start : start + width], gate_proj, up_proj, carry,
            positions(order, bits), start, c == len(chunks) - 1,
        )
    hidden = carry
    done = []
    for c, (start, width) in enumerate(chunks):
        order = bits if c % 2 == 0 else bits[::-1]
        near, far = leave(
            hidden, down_proj, row_gate, turned, positions(order, bits), start, width, block
        )
        buf = add(near, swap(far, "seq", 1))
        own = scatter_slabs(buf, order)
        moe = sum_half(own[half:], own[:half], n_exp)
        kept = (mixed_kept[c].astype(F32) + moe).astype(BF16)
        done.append((kept, swap(kept, "exp", 1)))
    mine = jnp.concatenate([d[0] for d in done], axis=1)
    theirs = jnp.concatenate([d[1] for d in done], axis=1)
    flipped = low_bit == 1
    return jnp.concatenate(
        [jnp.where(flipped, theirs, mine), jnp.where(flipped, mine, theirs)], axis=0
    )


def solution(mesh):
    return jax.shard_map(
        on_device,
        mesh=mesh,
        in_specs=(
            P("seq", "exp"),
            P("seq", None),
            P("seq", None),
            P("exp"),
            P("seq", None),
            P("exp", None),
            P(),
            P("seq", None),
            P("seq", None),
            P("seq", None, "exp"),
            P("seq", None, "exp"),
            P("seq", "exp", None),
        ),
        out_specs=P("seq", None),
        check_vma=False,
    )
```

time: 492 us -> 361 us (0.73)
  blocking collectives: 105 us -> 0 us
  Pallas kernels: 0 us -> 93.8 us
  waiting for transfers between devices: 217 us -> 150 us
  matrix products: 41.4 us -> 0 us
  starting transfers between devices: 12.3 us -> 49 us
  local copies, waits for them, and re-layouts: 62.8 us -> 44 us
  other arithmetic: 39 us -> 21.9 us
  between operations: 13.8 us -> 0.84 us
    ppermute x2 -> x52, waiting for transfers between devices: 0.01 us -> 150 us  [the longest x51 150 us: swap(): return lax.ppermute(x, axis, [(i, i ^ bit) for i in range(count)])]
    psum x2 -> x0, waiting for transfers between devices: 116 us -> none  [the longest x1 63.3 us: on_device(): lax.psum(moe_part.astype(jnp.bfloat16), 'exp').astype(jnp.float32)]
    all_to_all x1 -> x0, blocking collectives: 105 us -> none  [on_device(): lax.all_to_all(packed, 'seq', split_axis=0, concat_axis=0, tiled=True)]
    all_to_all x1 -> x0, waiting for transfers between devices: 101 us -> none  [send_back(): lax.all_to_all(partial_out, 'seq', split_axis=0, concat_axis=0, tiled=True)]
    pallas_call x0 -> x14, Pallas kernels: none -> 93.8 us  [the longest x4 41.5 us: enter(): pl.pallas_call(functools.partial(enter_kernel, first=first, last=total if...]
    ppermute x2 -> x52, starting transfers between devices: 6.9 us -> 49 us  [the longest x51 46.6 us: swap(): return lax.ppermute(x, axis, [(i, i ^ bit) for i in range(count)])]
    dot_general x5 -> x0, matrix products: 41.4 us -> none  [the longest x1 25.9 us: on_device(): jnp.einsum('secf,efd->secd', hidden, down_proj, preferred_element_type=jn...]
    gather x2 -> x0, local copies, waits for them, and re-layouts: 24.5 us -> none  [the longest x1 16.4 us: on_device(): flat_back[targets].astype(jnp.float32)]
  transfers between devices with their start and end apart: 5 -> 52, of which waited for: 3 -> 24; matrix products, arithmetic and copies ran while one was open for 4% -> 16% of each run, Pallas kernels for 0% -> 13%
where the time goes in v1:
time: 361 us; the launch traced here: 359 us
  waiting for transfers between devices  150 us (42%)
  Pallas kernels  93.8 us (26%)
  starting transfers between devices  49 us (14%)
  local copies, waits for them, and re-layouts  44 us (12%)
  other arithmetic  21.9 us (6%)
    ppermute x51, waiting for transfers between devices, swap(): return lax.ppermute(x, axis, [(i, i ^ bit) for i in range(count)])  150 us
    ppermute x51, starting transfers between devices, swap(): return lax.ppermute(x, axis, [(i, i ^ bit) for i in range(count)])  46.6 us
    pallas_call x4, Pallas kernels, enter(): pl.pallas_call(functools.partial(enter_kernel, first=first, last=total if...  41.5 us
    pallas_call x4, Pallas kernels, leave(): pl.pallas_call(functools.partial(leave_kernel, orders=orders, slabs=slabs...  29.7 us
    unnamed x65, local copies, waits for them, and re-layouts  26.1 us
    pallas_call x4, Pallas kernels, project(): pl.pallas_call(functools.partial(project_kernel, width=width), grid_spec=...  11.9 us
    concatenate x11, other arithmetic, gather_slabs(): buf = jnp.concatenate([buf, swap(buf, 'seq', bit)], axis=0)  10.5 us
    convert_element_type x20, other arithmetic, add(): return (a.astype(F32) + b.astype(F32)).astype(BF16)  8.59 us
  transfers between devices with their start and end apart: 52, of which 24 were waited for; matrix products, arithmetic and copies ran while one was open for 16% of the time, Pallas kernels for 13%

profile of v1, /device:TPU:0, one launch (start us, length us, event | category | flops | bytes accessed | tf_op | source)
XLA Modules:
  0.0 359.2 jit_solution(166301477731750441)
XLA Ops:
  6.5 8.5 %copy.50.w_ref = bf16[1024,2880]{1,0:T(8,128)(2,1)} copy(bf16[1024,2880]{0,1:T(8,128)(2,1)} %param.17) | data formatting | bytes 11796480 | tf_op args[5]
  17.2 7.8 %attention.1.ctx_ref = bf16[256,1024]{1,0:T(8,128)(2,1)} custom-call(s32[1]{0:T(128)} %bitcast.1.slab_ref, f32[16]{0:T(128)} %sink_ref.1, bf16[256,1024]{1,0:T(8,128)(2,1)} %q_ref.1, bf16[2,2,384,128]{3,2,1,0:T(8,128)(2,1)} %pad_maximum_fusion.10.k_ref, bf16[2,2,384,128]{3,2,1,0:T(8,128)(2,1)} %pad_maximum_fusion.11.v_ref), custom_call_target="tpu_custom_call" | custom-call | flops 4000000000 | bytes 2000000 | tf_op jit(solution)/shard_map/attention/pallas_call | solution.py:127
  27.9 3.0 project.7
  30.9 3.0 project.6
  33.9 3.1 project.4
  43.3 3.5 collective-permute-start.4
  47.5 3.5 collective-permute-start.19
  51.0 11.1 %collective-permute-done.1 = bf16[128,768]{1,0:T(8,128)(2,1)S(1)} collective-permute-done((bf16[128,768]{1,0:T(8,128)(2,1)S(1)}, bf16[128,768]{1,0:T(8,128)(2,1)S(1)}, u32[]{:S(2)}, u32[]{:S(2)}) %collective-permute-start.1) | collective-permute-done | bytes 196640 | tf_op jit(solution)/shard_map/ppermute | solution.py:37
  65.3 14.7 %collective-permute-done.2 = bf16[128,768]{1,0:T(8,128)(2,1)S(1)} collective-permute-done((bf16[128,768]{1,0:T(8,128)(2,1)S(1)}, bf16[128,768]{1,0:T(8,128)(2,1)S(1)}, u32[]{:S(2)}, u32[]{:S(2)}) %collective-permute-start.2) | collective-permute-done | bytes 196640 | tf_op jit(solution)/shard_map/ppermute | solution.py:37
  82.4 7.5 %collective-permute-done.24 = bf16[128,768]{1,0:T(8,128)(2,1)S(1)} collective-permute-done((bf16[128,768]{1,0:T(8,128)(2,1)S(1)}, bf16[128,768]{1,0:T(8,128)(2,1)S(1)}, u32[]{:S(2)}, u32[]{:S(2)}) %collective-permute-start.24) | collective-permute-done | bytes 196640 | tf_op jit(solution)/shard_map/ppermute | solution.py:37
  96.0 5.3 %collective-permute-done.25 = bf16[1,256,768]{2,1,0:T(8,128)(2,1)S(1)} collective-permute-done((bf16[1,256,768]{2,1,0:T(8,128)(2,1)S(1)}, bf16[1,256,768]{2,1,0:T(8,128)(2,1)S(1)}, u32[]{:S(2)}, u32[]{:S(2)}) %collective-permute-start.25) | collective-permute-done | bytes 393248 | tf_op jit(solution)/shard_map/ppermute | solution.py:37
  108.8 20.5 %collective-permute-done.6 = bf16[1,256,576]{2,1,0:T(8,128)(2,1)S(1)} collective-permute-done((bf16[1,256,576]{2,1,0:T(8,128)(2,1)S(1)}, bf16[1,256,576]{2,1,0:T(8,128)(2,1)S(1)}, u32[]{:S(2)}, u32[]{:S(2)}) %collective-permute-start.6) | collective-permute-done | bytes 294944 | tf_op jit(solution)/shard_map/ppermute | solution.py:37
  135.2 10.4 %collective-permute-done.7 = bf16[2,256,576]{1,2,0:T(8,128)(2,1)} collective-permute-done((bf16[2,256,576]{1,2,0:T(8,128)(2,1)}, bf16[2,256,576]{1,2,0:T(8,128)(2,1)}, u32[]{:S(2)}, u32[]{:S(2)}) %collective-permute-start.7) | collective-permute-done | bytes 589856 | tf_op jit(solution)/shard_map/ppermute | solution.py:37
  157.8 2.9 collective-permute-done.10
  161.8 16.4 %copy.58.w_ref = bf16[4,512,2880]{2,1,0:T(8,128)(2,1)} copy(bf16[4,512,2880]{1,2,0:T(8,128)(2,1)} %param.23) | data formatting | bytes 23592960 | tf_op args[11]
  184.2 9.5 %enter.4 = (f32[4,384,1024]{2,1,0:T(8,128)}, f32[4,384,128]{2,1,0:T(8,128)}) custom-call(bf16[4,256,768]{2,1,0:T(8,128)(2,1)} %copy-done.1, bf16[4,256,768]{2,1,0:T(8,128)(2,1)} %collective-permute-done.27.refs_1_, bf16[8,192,256]{2,1,0:T(8,128)(2,1)} %get-tuple-element.22.refs_2_, f32[1,768]{1,0:T(1,128)} %get-tuple-element.50.refs_3_, ...), custom_call_target="tpu_custom_call" | custom-call | flops 3623878656 | bytes 6291456 | tf_op jit(solution)/shard_map/enter/pallas_call | solution.py:267
  193.6 11.3 %enter.5 = (f32[4,384,1024]{2,1,0:T(8,128)}, f32[4,384,128]{2,1,0:T(8,128)}) custom-call(bf16[4,256,768]{2,1,0:T(8,128)(2,1)} %pad_maximum_fusion.1.refs_0_, bf16[4,256,768]{2,1,0:T(8,128)(2,1)} %collective-permute-done.23.refs_1_, bf16[8,192,256]{2,1,0:T(8,128)(2,1)} %get-tuple-element.22.refs_2_, ...), custom_call_target="tpu_custom_call", output_to_operand_aliasing={{0}: (6, {})} | custom-call | flops 3623878656 | bytes 6291456 | tf_op jit(solution)/shard_map/enter/pallas_call | solution.py:267
  205.0 11.1 %enter.6 = (f32[4,384,1024]{2,1,0:T(8,128)}, f32[4,384,128]{2,1,0:T(8,128)}) custom-call(bf16[4,256,768]{2,1,0:T(8,128)(2,1)} %pad_maximum_fusion.refs_0_, bf16[4,256,768]{2,1,0:T(8,128)(2,1)} %collective-permute-done.17.refs_1_, bf16[8,192,256]{2,1,0:T(8,128)(2,1)} %get-tuple-element.22.refs_2_, ...), custom_call_target="tpu_custom_call", output_to_operand_aliasing={{0}: (6, {})} | custom-call | flops 3623878656 | bytes 6291456 | tf_op jit(solution)/shard_map/enter/pallas_call | solution.py:267
  216.1 9.6 %enter.7.hidden_ref = bf16[4,384,512]{2,1,0:T(8,128)(2,1)} custom-call(bf16[4,256,576]{2,1,0:T(8,128)(2,1)} %copy-done, bf16[4,256,576]{2,1,0:T(8,128)(2,1)} %copy.57.refs_1_, bf16[8,192,256]{2,1,0:T(8,128)(2,1)} %get-tuple-element.22.refs_2_, f32[1,576]{1,0:T(1,128)} %slice.204.refs_3_, bf16[4,2880,512]{2,1,0:T(8,128)(2,1)} %refs_4_.7, ...), custom_call_target="tpu_custom_call" | custom-call | flops 2717908992 | bytes 4718592 | tf_op jit(solution)/shard_map/enter/pallas_call | solution.py:267
  225.7 7.0 %leave.7 = (bf16[4,256,576]{2,1,0:T(8,128)(2,1)}, bf16[4,256,576]{2,1,0:T(8,128)(2,1)}) custom-call(bf16[4,384,512]{2,1,0:T(8,128)(2,1)} %enter.7.hidden_ref, bf16[4,512,2880]{2,1,0:T(8,128)(2,1)} %copy.58.w_ref, f32[4,384,128]{2,1,0:T(8,128)} %get-tuple-element.29.gate_ref, bf16[8,256,192]{2,1,0:T(8,128)(2,1)} %get-tuple-element.30.turned_ref), custom_call_target="tpu_custom_call" | custom-call | flops 1358954496 | bytes 2359296 | tf_op jit(solution)/shard_map/leave/pallas_call | solution.py:320
  234.9 7.6 %leave.6 = (bf16[4,256,768]{2,1,0:T(8,128)(2,1)}, bf16[4,256,768]{2,1,0:T(8,128)(2,1)}) custom-call(bf16[4,384,512]{2,1,0:T(8,128)(2,1)} %enter.7.hidden_ref, bf16[4,512,2880]{2,1,0:T(8,128)(2,1)} %copy.58.w_ref, f32[4,384,128]{2,1,0:T(8,128)} %get-tuple-element.29.gate_ref, bf16[8,256,192]{2,1,0:T(8,128)(2,1)} %get-tuple-element.30.turned_ref), custom_call_target="tpu_custom_call" | custom-call | flops 1811939328 | bytes 3145728 | tf_op jit(solution)/shard_map/leave/pallas_call | solution.py:320
  246.3 7.5 %leave.5 = (bf16[4,256,768]{2,1,0:T(8,128)(2,1)}, bf16[4,256,768]{2,1,0:T(8,128)(2,1)}) custom-call(bf16[4,384,512]{2,1,0:T(8,128)(2,1)} %enter.7.hidden_ref, bf16[4,512,2880]{2,1,0:T(8,128)(2,1)} %copy.58.w_ref, f32[4,384,128]{2,1,0:T(8,128)} %get-tuple-element.29.gate_ref, bf16[8,256,192]{2,1,0:T(8,128)(2,1)} %get-tuple-element.30.turned_ref), custom_call_target="tpu_custom_call" | custom-call | flops 1811939328 | bytes 3145728 | tf_op jit(solution)/shard_map/leave/pallas_call | solution.py:320
  254.0 7.6 %leave.4 = (bf16[4,256,768]{2,1,0:T(8,128)(2,1)}, bf16[4,256,768]{2,1,0:T(8,128)(2,1)}) custom-call(bf16[4,384,512]{2,1,0:T(8,128)(2,1)} %enter.7.hidden_ref, bf16[4,512,2880]{2,1,0:T(8,128)(2,1)} %copy.58.w_ref, f32[4,384,128]{2,1,0:T(8,128)} %get-tuple-element.29.gate_ref, bf16[8,256,192]{2,1,0:T(8,128)(2,1)} %get-tuple-element.30.turned_ref), custom_call_target="tpu_custom_call" | custom-call | flops 1811939328 | bytes 3145728 | tf_op jit(solution)/shard_map/leave/pallas_call | solution.py:320
  266.5 6.6 %collective-permute-done.48 = bf16[1,256,576]{2,1,0:T(8,128)(2,1)S(1)} collective-permute-done((bf16[1,256,576]{2,1,0:T(8,128)(2,1)S(1)}, bf16[1,256,576]{2,1,0:T(8,128)(2,1)S(1)}, u32[]{:S(2)}, u32[]{:S(2)}) %collective-permute-start.48) | collective-permute-done | bytes 294944 | tf_op jit(solution)/shard_map/ppermute | solution.py:37
  282.0 4.7 %collective-permute-done.50 = bf16[128,576]{1,0:T(8,128)(2,1)S(1)} collective-permute-done((bf16[128,576]{1,0:T(8,128)(2,1)S(1)}, bf16[128,576]{1,0:T(8,128)(2,1)S(1)}, u32[]{:S(2)}, u32[]{:S(2)}) %collective-permute-start.50) | collective-permute-done | bytes 147488 | tf_op jit(solution)/shard_map/ppermute | solution.py:37
  286.8 3.1 collective-permute-done.41
  291.2 3.8 %collective-permute-done.35 = bf16[2,256,768]{2,1,0:T(8,128)(2,1)S(1)} collective-permute-done((bf16[2,256,768]{2,1,0:T(8,128)(2,1)S(1)}, bf16[2,256,768]{2,1,0:T(8,128)(2,1)S(1)}, u32[]{:S(2)}, u32[]{:S(2)}) %collective-permute-start.35) | collective-permute-done | bytes 786464 | tf_op jit(solution)/shard_map/ppermute | solution.py:37
  296.1 10.6 %collective-permute-done.29 = bf16[2,256,768]{2,1,0:T(8,128)(2,1)S(1)} collective-permute-done((bf16[2,256,768]{2,1,0:T(8,128)(2,1)S(1)}, bf16[2,256,768]{2,1,0:T(8,128)(2,1)S(1)}, u32[]{:S(2)}, u32[]{:S(2)}) %collective-permute-start.29) | collective-permute-done | bytes 786464 | tf_op jit(solution)/shard_map/ppermute | solution.py:37
  308.3 6.1 %collective-permute-done.36 = bf16[1,256,768]{2,1,0:T(8,128)(2,1)S(1)} collective-permute-done((bf16[1,256,768]{2,1,0:T(8,128)(2,1)S(1)}, bf16[1,256,768]{2,1,0:T(8,128)(2,1)S(1)}, u32[]{:S(2)}, u32[]{:S(2)}) %collective-permute-start.36) | collective-permute-done | bytes 393248 | tf_op jit(solution)/shard_map/ppermute | solution.py:37
  319.4 8.9 %collective-permute-done.37 = bf16[128,768]{1,0:T(8,128)(2,1)S(1)} collective-permute-done((bf16[128,768]{1,0:T(8,128)(2,1)S(1)}, bf16[128,768]{1,0:T(8,128)(2,1)S(1)}, u32[]{:S(2)}, u32[]{:S(2)}) %collective-permute-start.37) | collective-permute-done | bytes 196640 | tf_op jit(solution)/shard_map/ppermute | solution.py:37
  331.4 11.0 %collective-permute-done.38 = bf16[128,768]{1,0:T(8,128)(2,1)S(1)} collective-permute-done((bf16[128,768]{1,0:T(8,128)(2,1)S(1)}, bf16[128,768]{1,0:T(8,128)(2,1)S(1)}, u32[]{:S(2)}, u32[]{:S(2)}) %collective-permute-start.38) | collective-permute-done | bytes 196640 | tf_op jit(solution)/shard_map/ppermute | solution.py:37
  347.0 7.6 %collective-permute-done.33 = bf16[128,768]{1,0:T(8,128)(2,1)S(1)} collective-permute-done((bf16[128,768]{1,0:T(8,128)(2,1)S(1)}, bf16[128,768]{1,0:T(8,128)(2,1)S(1)}, u32[]{:S(2)}, u32[]{:S(2)}) %collective-permute-start.33) | collective-permute-done | bytes 196640 | tf_op jit(solution)/shard_map/ppermute | solution.py:37
  (243 shorter events, 103.7 us)
Async XLA Ops:
  39.5 24.6 %collective-permute-start.12 = (bf16[128,768]{1,0:T(8,128)(2,1)S(1)}, bf16[128,768]{1,0:T(8,128)(2,1)S(1)}, u32[]{:S(2)}, u32[]{:S(2)}) collective-permute-start(bf16[128,768]{1,0:T(8,128)(2,1)S(1)} %slice_bitcast_fusion.8), channel_id=1, source_target_pairs={{0,1},{1,0},{2,3},{3,2},{4,5},{5,4},{6,7},{7,6},{8,9},{9,8},{10,11... | collective-permute-start | bytes 589832 | tf_op jit(solution)/shard_map/ppermute | solution.py:37
  42.6 19.6 %collective-permute-start.1 = (bf16[128,768]{1,0:T(8,128)(2,1)S(1)}, bf16[128,768]{1,0:T(8,128)(2,1)S(1)}, u32[]{:S(2)}, u32[]{:S(2)}) collective-permute-start(bf16[128,768]{1,0:T(8,128)(2,1)S(1)} %slice_bitcast_fusion.10), channel_id=1, source_target_pairs={{0,1},{1,0},{2,3},{3,2},{4,5},{5,4},{6,7},{7,6},{8,9},{9,8},{10,11... | collective-permute-start | bytes 589832 | tf_op jit(solution)/shard_map/ppermute | solution.py:37
  43.3 48.3 %collective-permute-start.4 = (bf16[128,576]{1,0:T(8,128)(2,1)S(1)}, bf16[128,576]{1,0:T(8,128)(2,1)S(1)}, u32[]{:S(2)}, u32[]{:S(2)}) collective-permute-start(bf16[128,576]{1,0:T(8,128)(2,1)S(1)} %fusion.7), channel_id=1, source_target_pairs={{0,2},{1,3},{2,0},{3,1},{4,6},{5,7},{6,4},{7,5},{8,10},{9,11},{10,... | collective-permute-start | bytes 442376 | tf_op jit(solution)/shard_map/ppermute | solution.py:37
  47.5 32.7 %collective-permute-start.19 = (bf16[128,768]{1,0:T(8,128)(2,1)S(1)}, bf16[128,768]{1,0:T(8,128)(2,1)S(1)}, u32[]{:S(2)}, u32[]{:S(2)}) collective-permute-start(bf16[128,768]{1,0:T(8,128)(2,1)S(1)} %fusion.3), channel_id=1, source_target_pairs={{0,2},{1,3},{2,0},{3,1},{4,6},{5,7},{6,4},{7,5},{8,10},{9,11},{10,... | collective-permute-start | bytes 589832 | tf_op jit(solution)/shard_map/ppermute | solution.py:37
  62.2 17.8 %collective-permute-start.2 = (bf16[128,768]{1,0:T(8,128)(2,1)S(1)}, bf16[128,768]{1,0:T(8,128)(2,1)S(1)}, u32[]{:S(2)}, u32[]{:S(2)}) collective-permute-start(bf16[128,768]{1,0:T(8,128)(2,1)S(1)} %fusion.5), channel_id=1, source_target_pairs={{0,2},{1,3},{2,0},{3,1},{4,6},{5,7},{6,4},{7,5},{8,10},{9,11},{10,... | collective-permute-start | bytes 589832 | tf_op jit(solution)/shard_map/ppermute | solution.py:37
  64.2 31.6 %collective-permute-start.13 = (bf16[128,768]{1,0:T(8,128)(2,1)S(1)}, bf16[128,768]{1,0:T(8,128)(2,1)S(1)}, u32[]{:S(2)}, u32[]{:S(2)}) collective-permute-start(bf16[128,768]{1,0:T(8,128)(2,1)S(1)} %fusion.4), channel_id=1, source_target_pairs={{0,2},{1,3},{2,0},{3,1},{4,6},{5,7},{6,4},{7,5},{8,10},{9,11},{10,... | collective-permute-start | bytes 589832 | tf_op jit(solution)/shard_map/ppermute | solution.py:37
  80.3 13.7 %collective-permute-start.20 = (bf16[128,768]{1,0:T(8,128)(2,1)S(1)}, bf16[128,768]{1,0:T(8,128)(2,1)S(1)}, u32[]{:S(2)}, u32[]{:S(2)}) collective-permute-start(bf16[128,768]{1,0:T(8,128)(2,1)S(1)} %add_convert_fusion.15), channel_id=1, source_target_pairs={{0,1},{1,0},{2,3},{3,2},{4,5},{5,4},{6,7},{7,6},{8,9},{9,8},{10,11... | collective-permute-start | bytes 589832 | tf_op jit(solution)/shard_map/ppermute | solution.py:37
  102.3 31.2 %collective-permute-start.26 = (bf16[2,256,768]{2,1,0:T(8,128)(2,1)}, bf16[2,256,768]{2,1,0:T(8,128)(2,1)}, u32[]{:S(2)}, u32[]{:S(2)}) collective-permute-start(bf16[2,256,768]{2,1,0:T(8,128)(2,1)} %pad_maximum_fusion.7), channel_id=1, source_target_pairs={{0,16},{4,20},{8,24},{12,28},{16,0},{20,4},{24,8},{28,12},{1,17},{... | collective-permute-start | bytes 2359304 | tf_op jit(solution)/shard_map/ppermute | solution.py:37
  104.0 25.2 %collective-permute-start.6 = (bf16[1,256,576]{2,1,0:T(8,128)(2,1)S(1)}, bf16[1,256,576]{2,1,0:T(8,128)(2,1)S(1)}, u32[]{:S(2)}, u32[]{:S(2)}) collective-permute-start(bf16[1,256,576]{2,1,0:T(8,128)(2,1)S(1)} %maximum_bitcast_fusion.3), channel_id=1, source_target_pairs={{0,16},{4,20},{8,24},{12,28},{16,0},{20,4},{24,8},{28,12},{1,17},{... | collective-permute-start | bytes 884744 | tf_op jit(solution)/shard_map/ppermute | solution.py:37
  104.5 27.7 %collective-permute-start.15 = (bf16[1,256,768]{2,1,0:T(8,128)(2,1)S(1)}, bf16[1,256,768]{2,1,0:T(8,128)(2,1)S(1)}, u32[]{:S(2)}, u32[]{:S(2)}) collective-permute-start(bf16[1,256,768]{2,1,0:T(8,128)(2,1)S(1)} %maximum_bitcast_fusion), channel_id=1, source_target_pairs={{0,8},{4,12},{8,0},{12,4},{16,24},{20,28},{24,16},{28,20},{1,9},{5... | collective-permute-start | bytes 1179656 | tf_op jit(solution)/shard_map/ppermute | solution.py:37
  107.2 40.5 %collective-permute-start.22 = (bf16[2,256,768]{2,1,0:T(8,128)(2,1)}, bf16[2,256,768]{2,1,0:T(8,128)(2,1)}, u32[]{:S(2)}, u32[]{:S(2)}) collective-permute-start(bf16[2,256,768]{2,1,0:T(8,128)(2,1)} %pad_maximum_fusion.6), channel_id=1, source_target_pairs={{0,8},{4,12},{8,0},{12,4},{16,24},{20,28},{24,16},{28,20},{1,9},{5... | collective-permute-start | bytes 2359304 | tf_op jit(solution)/shard_map/ppermute | solution.py:37
  130.4 15.1 %collective-permute-start.7 = (bf16[2,256,576]{1,2,0:T(8,128)(2,1)}, bf16[2,256,576]{1,2,0:T(8,128)(2,1)}, u32[]{:S(2)}, u32[]{:S(2)}) collective-permute-start(bf16[2,256,576]{1,2,0:T(8,128)(2,1)} %copy.52), channel_id=1, source_target_pairs={{0,8},{4,12},{8,0},{12,4},{16,24},{20,28},{24,16},{28,20},{1,9},{5... | collective-permute-start | bytes 1769480 | tf_op jit(solution)/shard_map/ppermute | solution.py:37
  133.2 21.0 %collective-permute-start.16 = (bf16[2,256,768]{2,1,0:T(8,128)(2,1)}, bf16[2,256,768]{2,1,0:T(8,128)(2,1)}, u32[]{:S(2)}, u32[]{:S(2)}) collective-permute-start(bf16[2,256,768]{2,1,0:T(8,128)(2,1)} %pad_maximum_fusion.5), channel_id=1, source_target_pairs={{0,16},{4,20},{8,24},{12,28},{16,0},{20,4},{24,8},{28,12},{1,17},{... | collective-permute-start | bytes 2359304 | tf_op jit(solution)/shard_map/ppermute | solution.py:37
  135.0 49.2 %collective-permute-start.27 = (bf16[4,256,768]{2,1,0:T(8,128)(2,1)S(1)}, bf16[4,256,768]{2,1,0:T(8,128)(2,1)}, u32[]{:S(2)}, u32[]{:S(2)}) collective-permute-start(bf16[4,256,768]{2,1,0:T(8,128)(2,1)S(1)} %pad_maximum_fusion.2.refs_0_), channel_id=1, source_target_pairs={{0,4},{4,0},{8,12},{12,8},{16,20},{20,16},{24,28},{28,24},{1,5},{5... | collective-permute-start | bytes 4718600 | tf_op jit(solution)/shard_map/ppermute | solution.py:37
  150.3 43.4 %collective-permute-start.23 = (bf16[4,256,768]{2,1,0:T(8,128)(2,1)}, bf16[4,256,768]{2,1,0:T(8,128)(2,1)}, u32[]{:S(2)}, u32[]{:S(2)}) collective-permute-start(bf16[4,256,768]{2,1,0:T(8,128)(2,1)} %pad_maximum_fusion.1.refs_0_), channel_id=1, source_target_pairs={{0,4},{4,0},{8,12},{12,8},{16,20},{20,16},{24,28},{28,24},{1,5},{5... | collective-permute-start | bytes 4718600 | tf_op jit(solution)/shard_map/ppermute | solution.py:37
  152.0 29.7 %collective-permute-start.8 = (bf16[4,256,576]{1,2,0:T(8,128)(2,1)}, bf16[4,256,576]{1,2,0:T(8,128)(2,1)}, u32[]{:S(2)}, u32[]{:S(2)}) collective-permute-start(bf16[4,256,576]{1,2,0:T(8,128)(2,1)} %copy.54), channel_id=1, source_target_pairs={{0,4},{4,0},{8,12},{12,8},{16,20},{20,16},{24,28},{28,24},{1,5},{5... | collective-permute-start | bytes 3538952 | tf_op jit(solution)/shard_map/ppermute | solution.py:37
  156.8 48.2 %collective-permute-start.17 = (bf16[4,256,768]{2,1,0:T(8,128)(2,1)}, bf16[4,256,768]{2,1,0:T(8,128)(2,1)}, u32[]{:S(2)}, u32[]{:S(2)}) collective-permute-start(bf16[4,256,768]{2,1,0:T(8,128)(2,1)} %pad_maximum_fusion.refs_0_), channel_id=1, source_target_pairs={{0,4},{4,0},{8,12},{12,8},{16,20},{20,16},{24,28},{28,24},{1,5},{5... | collective-permute-start | bytes 4718600 | tf_op jit(solution)/shard_map/ppermute | solution.py:37
  160.6 17.6 %collective-permute-start.11 = (f32[4,8,256]{2,1,0:T(8,128)S(1)}, f32[4,8,256]{2,1,0:T(8,128)S(1)}, u32[]{:S(2)}, u32[]{:S(2)}) collective-permute-start(f32[4,8,256]{2,1,0:T(8,128)S(1)} %pad_maximum_fusion.16), channel_id=1, source_target_pairs={{0,4},{4,0},{8,12},{12,8},{16,20},{20,16},{24,28},{28,24},{1,5},{5... | collective-permute-start | bytes 98312 | tf_op jit(solution)/shard_map/ppermute | solution.py:37
  242.5 20.8 %collective-permute-start.40 = (bf16[4,256,768]{2,1,0:T(8,128)(2,1)}, bf16[4,256,768]{2,1,0:T(8,128)(2,1)}, u32[]{:S(2)}, u32[]{:S(2)}) collective-permute-start(bf16[4,256,768]{2,1,0:T(8,128)(2,1)} %get-tuple-element.36), channel_id=1, source_target_pairs={{0,4},{4,0},{8,12},{12,8},{16,20},{20,16},{24,28},{28,24},{1,5},{5... | collective-permute-start | bytes 4718600 | tf_op jit(solution)/shard_map/ppermute | solution.py:37
  245.2 16.7 %collective-permute-start.47 = (bf16[2,256,576]{1,2,0:T(8,128)(2,1)S(1)}, bf16[2,256,576]{1,2,0:T(8,128)(2,1)S(1)}, u32[]{:S(2)}, u32[]{:S(2)}) collective-permute-start(bf16[2,256,576]{1,2,0:T(8,128)(2,1)S(1)} %copy.64), channel_id=1, source_target_pairs={{0,8},{4,12},{8,0},{12,4},{16,24},{20,28},{24,16},{28,20},{1,9},{5... | collective-permute-start | bytes 1769480 | tf_op jit(solution)/shard_map/ppermute | solution.py:37
  253.8 19.5 %collective-permute-start.34 = (bf16[4,256,768]{2,1,0:T(8,128)(2,1)}, bf16[4,256,768]{2,1,0:T(8,128)(2,1)}, u32[]{:S(2)}, u32[]{:S(2)}) collective-permute-start(bf16[4,256,768]{2,1,0:T(8,128)(2,1)} %get-tuple-element.34), channel_id=1, source_target_pairs={{0,4},{4,0},{8,12},{12,8},{16,20},{20,16},{24,28},{28,24},{1,5},{5... | collective-permute-start | bytes 4718600 | tf_op jit(solution)/shard_map/ppermute | solution.py:37
  261.6 17.5 %collective-permute-start.28 = (bf16[4,256,768]{2,1,0:T(8,128)(2,1)}, bf16[4,256,768]{2,1,0:T(8,128)(2,1)}, u32[]{:S(2)}, u32[]{:S(2)}) collective-permute-start(bf16[4,256,768]{2,1,0:T(8,128)(2,1)} %get-tuple-element.32), channel_id=1, source_target_pairs={{0,4},{4,0},{8,12},{12,8},{16,20},{20,16},{24,28},{28,24},{1,5},{5... | collective-permute-start | bytes 4718600 | tf_op jit(solution)/shard_map/ppermute | solution.py:37
  265.5 24.4 %collective-permute-start.41 = (bf16[2,256,768]{2,1,0:T(8,128)(2,1)S(1)}, bf16[2,256,768]{2,1,0:T(8,128)(2,1)S(1)}, u32[]{:S(2)}, u32[]{:S(2)}) collective-permute-start(bf16[2,256,768]{2,1,0:T(8,128)(2,1)S(1)} %slice.225), channel_id=1, source_target_pairs={{0,16},{4,20},{8,24},{12,28},{16,0},{20,4},{24,8},{28,12},{1,17},{... | collective-permute-start | bytes 2359304 | tf_op jit(solution)/shard_map/ppermute | solution.py:37
  275.1 19.9 %collective-permute-start.35 = (bf16[2,256,768]{2,1,0:T(8,128)(2,1)S(1)}, bf16[2,256,768]{2,1,0:T(8,128)(2,1)S(1)}, u32[]{:S(2)}, u32[]{:S(2)}) collective-permute-start(bf16[2,256,768]{2,1,0:T(8,128)(2,1)S(1)} %slice.219), channel_id=1, source_target_pairs={{0,8},{4,12},{8,0},{12,4},{16,24},{20,28},{24,16},{28,20},{1,9},{5... | collective-permute-start | bytes 2359304 | tf_op jit(solution)/shard_map/ppermute | solution.py:37
  281.0 25.7 %collective-permute-start.29 = (bf16[2,256,768]{2,1,0:T(8,128)(2,1)S(1)}, bf16[2,256,768]{2,1,0:T(8,128)(2,1)S(1)}, u32[]{:S(2)}, u32[]{:S(2)}) collective-permute-start(bf16[2,256,768]{2,1,0:T(8,128)(2,1)S(1)} %slice.213), channel_id=1, source_target_pairs={{0,16},{4,20},{8,24},{12,28},{16,0},{20,4},{24,8},{28,12},{1,17},{... | collective-permute-start | bytes 2359304 | tf_op jit(solution)/shard_map/ppermute | solution.py:37
  286.7 70.6 %collective-permute-start.51 = (bf16[128,576]{1,0:T(8,128)(2,1)S(1)}, bf16[128,576]{1,0:T(8,128)(2,1)S(1)}, u32[]{:S(2)}, u32[]{:S(2)}) collective-permute-start(bf16[128,576]{1,0:T(8,128)(2,1)S(1)} %add_convert_fusion.18), channel_id=1, source_target_pairs={{0,1},{1,0},{2,3},{3,2},{4,5},{5,4},{6,7},{7,6},{8,9},{9,8},{10,11... | collective-permute-start | bytes 442376 | tf_op jit(solution)/shard_map/ppermute | solution.py:37
  290.1 17.9 %collective-permute-start.42 = (bf16[1,256,768]{2,1,0:T(8,128)(2,1)S(1)}, bf16[1,256,768]{2,1,0:T(8,128)(2,1)S(1)}, u32[]{:S(2)}, u32[]{:S(2)}) collective-permute-start(bf16[1,256,768]{2,1,0:T(8,128)(2,1)S(1)} %slice.227), channel_id=1, source_target_pairs={{0,8},{4,12},{8,0},{12,4},{16,24},{20,28},{24,16},{28,20},{1,9},{5... | collective-permute-start | bytes 1179656 | tf_op jit(solution)/shard_map/ppermute | solution.py:37
  295.2 19.2 %collective-permute-start.36 = (bf16[1,256,768]{2,1,0:T(8,128)(2,1)S(1)}, bf16[1,256,768]{2,1,0:T(8,128)(2,1)S(1)}, u32[]{:S(2)}, u32[]{:S(2)}) collective-permute-start(bf16[1,256,768]{2,1,0:T(8,128)(2,1)S(1)} %slice.221), channel_id=1, source_target_pairs={{0,16},{4,20},{8,24},{12,28},{16,0},{20,4},{24,8},{28,12},{1,17},{... | collective-permute-start | bytes 1179656 | tf_op jit(solution)/shard_map/ppermute | solution.py:37
  316.8 14.1 %collective-permute-start.31 = (bf16[128,768]{1,0:T(8,128)(2,1)S(1)}, bf16[128,768]{1,0:T(8,128)(2,1)S(1)}, u32[]{:S(2)}, u32[]{:S(2)}) collective-permute-start(bf16[128,768]{1,0:T(8,128)(2,1)S(1)} %slice_bitcast_fusion.4), channel_id=1, source_target_pairs={{0,1},{1,0},{2,3},{3,2},{4,5},{5,4},{6,7},{7,6},{8,9},{9,8},{10,11... | collective-permute-start | bytes 589832 | tf_op jit(solution)/shard_map/ppermute | solution.py:37
  316.9 28.0 %collective-permute-start.44 = (bf16[128,768]{1,0:T(8,128)(2,1)S(1)}, bf16[128,768]{1,0:T(8,128)(2,1)S(1)}, u32[]{:S(2)}, u32[]{:S(2)}) collective-permute-start(bf16[128,768]{1,0:T(8,128)(2,1)S(1)} %fusion), channel_id=1, source_target_pairs={{0,2},{1,3},{2,0},{3,1},{4,6},{5,7},{6,4},{7,5},{8,10},{9,11},{10,... | collective-permute-start | bytes 589832 | tf_op jit(solution)/shard_map/ppermute | solution.py:37
  328.3 14.2 %collective-permute-start.38 = (bf16[128,768]{1,0:T(8,128)(2,1)S(1)}, bf16[128,768]{1,0:T(8,128)(2,1)S(1)}, u32[]{:S(2)}, u32[]{:S(2)}) collective-permute-start(bf16[128,768]{1,0:T(8,128)(2,1)S(1)} %fusion.1), channel_id=1, source_target_pairs={{0,2},{1,3},{2,0},{3,1},{4,6},{5,7},{6,4},{7,5},{8,10},{9,11},{10,... | collective-permute-start | bytes 589832 | tf_op jit(solution)/shard_map/ppermute | solution.py:37
  330.9 13.8 %collective-permute-start.32 = (bf16[128,768]{1,0:T(8,128)(2,1)S(1)}, bf16[128,768]{1,0:T(8,128)(2,1)S(1)}, u32[]{:S(2)}, u32[]{:S(2)}) collective-permute-start(bf16[128,768]{1,0:T(8,128)(2,1)S(1)} %fusion.2), channel_id=1, source_target_pairs={{0,2},{1,3},{2,0},{3,1},{4,6},{5,7},{6,4},{7,5},{8,10},{9,11},{10,... | collective-permute-start | bytes 589832 | tf_op jit(solution)/shard_map/ppermute | solution.py:37
  (47 other events, 460.1 us)
